TPU v7x, 256 devices: a whole 4x4x8 slice. The times are simulated.
256 devices in a mesh: exp: 32 (over x, y, core), tp: 8 (over z).
Axes of the slice: x: 4, y: 4, z: 8, core: 2. Of those that a mesh axis runs over, the one named last changes fastest.
Arguments:
- tokens: bfloat16 [896, 4096], P('exp', 'tp'), may hold values from -6 to 6
- cotangent: bfloat16 [896, 4096], P('exp', 'tp'), may hold values from -6 to 6
- experts: int32 [896, 2], P('exp'), may hold values from 0 to 7, all different within a row; in each aligned block of 28 rows (0 to 27, 28 to 55, ...) at most 8 rows name the same one
- gates: float32 [896, 2], P('exp'), may hold values from 0.1 to 0.9
- w_gate: bfloat16 [32, 4096, 2048], P('exp', None, 'tp'), may hold values from -0.09375 to 0.09375
- w_up: bfloat16 [32, 4096, 2048], P('exp', None, 'tp'), may hold values from -0.09375 to 0.09375
- w_down: bfloat16 [32, 2048, 4096], P('exp', 'tp'), may hold values from -0.0625 to 0.0625
Outputs:
- output: bfloat16 [896, 4096], P('exp', 'tp')
- input_grad: bfloat16 [896, 4096], P('exp', 'tp')
- grad_gate: bfloat16 [32, 4096, 2048], P('exp', None, 'tp')
- grad_up: bfloat16 [32, 4096, 2048], P('exp', None, 'tp')
- grad_down: bfloat16 [32, 2048, 4096], P('exp', 'tp')
Inputs may be any that keep to these rules, and one draw needn't show every extreme that they name: Each row names 2 different experts. In each aligned block of 28 rows (the rows of one index of exp) no expert is named by more than 8 rows, and in some blocks one is named by exactly 8.
All inputs are finite; a program needn't handle non-finite values.
Results may differ from a plain program's by a relative error of at most 0.017.
Values may be sent and summed in bfloat16 or wider, within the bound.
No kernel may reach another device: no remote copies, remote signals or barrier semaphores. Data moves between devices by JAX's collectives and lax.ppermute only.
A program may use at most 64 MiB of HBM per device.

v0:
```python
import jax
import jax.numpy as jnp
from jax import lax
from jax.sharding import PartitionSpec as P

EXPERTS = 8
CAP = 8


def side_by_side(arrays, axis, split_dim, concat_dim, along):
    widths = [a.shape[along] for a in arrays]
    both = jnp.concatenate(arrays, axis=along)
    result = lax.all_to_all(both, axis, split_axis=split_dim, concat_axis=concat_dim, tiled=True)
    return tuple(jnp.split(result, [sum(widths[:k]) for k in range(1, len(widths))], axis=along))


def in_one_piece(arrays, axis, dim, along):
    both = jnp.concatenate(arrays, axis=along)
    result, at, done = (lax.all_gather(both, axis, axis=dim, tiled=True), 0, [])
    for a in arrays:
        done.append(lax.slice_in_dim(result, at, at + a.shape[along], axis=along))
        at += a.shape[along]
    return tuple(done)


def contract_rows(left, right):
    return lax.dot_general(
        left, right, (((0,), (0,)), ((), ())), preferred_element_type=jnp.float32
    )


def contract_cols(left, right):
    return lax.dot_general(
        left, right, (((1,), (1,)), ((), ())), preferred_element_type=jnp.float32
    )


def slot_places(experts, capacity):
    pair_ids = experts.reshape(-1)
    matches = (pair_ids[:, None] == jnp.arange(EXPERTS, dtype=jnp.int32)[None, :]).astype(jnp.int32)
    before = jnp.cumsum(matches, axis=0) - matches
    slot_ids = jnp.sum(before * matches, axis=1)
    return pair_ids * capacity + slot_ids


def per_device(tokens, cotangent, experts, gates, w_gate, w_up, w_down):
    exp_devices = lax.axis_size("exp")
    group_size = exp_devices // EXPERTS
    capacity = CAP
    tok_rows, top_count = experts.shape
    gate_mat = w_gate[0]
    up_mat = w_up[0]
    down_mat = w_down[0]
    row_count = exp_devices * capacity
    places = slot_places(experts, capacity)
    pick_table = (
        places[:, None] == jnp.arange(EXPERTS * capacity, dtype=jnp.int32)[None, :]
    ).astype(jnp.float32)
    per_token = pick_table.reshape(tok_rows, top_count, EXPERTS * capacity)
    weighted = jnp.sum(per_token * gates[:, :, None], axis=1)
    unweighted = jnp.sum(per_token, axis=1)
    pick_low = pick_table.astype(jnp.bfloat16)
    scaled = (gates[:, :, None] * cotangent[:, None, :].astype(jnp.float32)).astype(jnp.bfloat16)
    scaled = scaled.reshape(tok_rows * top_count, cotangent.shape[1])

    def merge_group(received):
        col_count = received.shape[2]
        summed = jnp.sum(received.reshape(EXPERTS, group_size, capacity, col_count), axis=1)
        return summed.reshape(EXPERTS * capacity, col_count)

    def gather_tokens(table, received):
        return jnp.dot(table, merge_group(received), preferred_element_type=jnp.float32)

    col_count = tokens.shape[1]
    repeated = jnp.repeat(tokens, top_count, axis=0)
    token_send = contract_rows(pick_low, repeated).astype(jnp.bfloat16)
    grad_send = contract_rows(pick_low, scaled).astype(jnp.bfloat16)
    token_send = jnp.broadcast_to(
        token_send.reshape(EXPERTS, 1, capacity, col_count),
        (EXPERTS, group_size, capacity, col_count),
    )
    grad_send = jnp.broadcast_to(
        grad_send.reshape(EXPERTS, 1, capacity, col_count),
        (EXPERTS, group_size, capacity, col_count),
    )
    token_send, grad_send = (
        token_send.reshape(exp_devices, capacity, col_count),
        grad_send.reshape(exp_devices, capacity, col_count),
    )
    token_part, grad_part = side_by_side((token_send, grad_send), "exp", 0, 0, 1)
    token_part = token_part.reshape(row_count, tokens.shape[1])
    grad_part = grad_part.reshape(row_count, tokens.shape[1])
    token_piece, grad_piece = in_one_piece((token_part, grad_part), "tp", 1, 0)
    first = jnp.dot(token_piece, gate_mat, preferred_element_type=jnp.float32)
    second = jnp.dot(token_piece, up_mat, preferred_element_type=jnp.float32)
    third = contract_cols(grad_piece, down_mat)
    sigmoid_gate = jax.nn.sigmoid(first)
    activation = (first * sigmoid_gate * second).astype(jnp.bfloat16)
    out_term = jnp.dot(activation, down_mat, preferred_element_type=jnp.float32)
    out_share = lax.psum_scatter(out_term, "tp", scatter_dimension=1, tiled=True)
    grad_first = (third * second * sigmoid_gate * (1.0 + first * (1.0 - sigmoid_gate))).astype(
        jnp.bfloat16
    )
    grad_second = (third * first * sigmoid_gate).astype(jnp.bfloat16)
    grad_down = contract_rows(activation, grad_piece).astype(jnp.bfloat16)
    grad_gate = contract_rows(token_piece, grad_first).astype(jnp.bfloat16)
    grad_up = contract_rows(token_piece, grad_second).astype(jnp.bfloat16)
    back_term = contract_cols(grad_first, gate_mat) + contract_cols(grad_second, up_mat)
    back_share = lax.psum_scatter(
        back_term.astype(jnp.bfloat16), "tp", scatter_dimension=1, tiled=True
    ).astype(jnp.float32)
    col_count = back_share.shape[1]
    out_back, grad_back = tuple(
        (
            part.astype(jnp.float32)
            for part in side_by_side(
                (
                    out_share.reshape(exp_devices, capacity, col_count).astype(jnp.bfloat16),
                    back_share.reshape(exp_devices, capacity, col_count).astype(jnp.bfloat16),
                ),
                "exp",
                0,
                0,
                1,
            )
        )
    )
    output = gather_tokens(weighted, out_back)
    input_grad = gather_tokens(unweighted, grad_back)
    return (
        output.astype(jnp.bfloat16),
        input_grad.astype(jnp.bfloat16),
        grad_gate[None],
        grad_up[None],
        grad_down[None],
    )


def solution(mesh):
    in_specs = (
        P("exp", "tp"),
        P("exp", "tp"),
        P("exp", None),
        P("exp", None),
        P("exp", None, "tp"),
        P("exp", None, "tp"),
        P("exp", "tp", None),
    )
    out_specs = (
        P("exp", "tp"),
        P("exp", "tp"),
        P("exp", None, "tp"),
        P("exp", None, "tp"),
        P("exp", "tp", None),
    )
    return jax.shard_map(
        per_device, mesh=mesh, in_specs=in_specs, out_specs=out_specs, check_vma=False
    )
```

profile of v0, /device:TPU:1, one launch (start us, length us, event | category | flops | bytes accessed | tf_op | source)
XLA Modules:
  0.0 223.3 jit_solution(2887709709159411879)
XLA Ops:
  7.2 0.0 copy-start
  7.2 0.0 all-gather.2.cloned.1.call-start
  7.2 0.9 copy.27
  8.1 0.1 eq.35
  8.2 0.1 fusion.26
  8.3 0.1 reduce_window_sum.11
  8.4 0.2 select_reduce_fusion.1
  8.6 0.8 copy.30
  9.4 0.8 mul.77
  10.2 0.1 mul.78
  10.3 0.1 mul.75
  10.4 0.8 broadcast_in_dim.32
  11.2 0.3 fusion.21
  11.5 0.3 fusion.22
  11.8 0.1 pad_maximum_fusion
  11.8 20.0 %all_to_all.10 = bf16[32,16,512]{2,1,0:T(8,128)(2,1)S(1)} all-to-all(bf16[32,16,512]{2,1,0:T(8,128)(2,1)S(1)} %pad_maximum_fusion), channel_id=1, replica_groups=mesh['exp'=32,'tp'=8] {'exp'}, dimensions={0} | all-to-all | bytes 1048576 | tf_op jit(solution)/shard_map/all_to_all | solution.py:13
  31.9 0.8 pad_maximum_fusion.1
  32.7 0.0 all-gather.2.cloned.1.call-update
  32.7 0.0 reduce-scatter.3.cloned.1.call-start
  32.8 53.5 %all-gather.2.cloned.1.call-done = bf16[512,4096]{1,0:T(8,128)(2,1)} async-done(((bf16[512,512]{1,0:T(8,128)(2,1)}), bf16[512,4096]{1,0:T(8,128)(2,1)}) %all-gather.2.cloned.1.call-update) | async-done | bytes 4194320 | tf_op jit(solution)/shard_map/all_gather | solution.py:19
  86.3 0.0 copy-start.1
  86.3 3.1 %fusion.13 = f32[256,256]{1,0:T(8,128)S(1)} fusion(bf16[1,4096,256]{2,1,0:T(8,128)(2,1)} %param.11, bf16[512,4096]{1,0:T(8,128)(2,1)} %all-gather.2.cloned.1.call-done), kind=kOutput, calls=%fused_computation.17 | convolution fusion | flops 536870912 | bytes 4456448 | tf_op jit(solution)/shard_map/dot_general | solution.py:94
  89.4 0.0 copy-done.1
  89.4 0.0 copy-start.2
  89.4 2.5 %fusion.4 = f32[256,256]{1,0:T(8,128)S(1)} fusion(bf16[1,256,4096]{2,1,0:T(8,128)(2,1)S(1)} %copy-done.1, bf16[512,4096]{1,0:T(8,128)(2,1)} %all-gather.2.cloned.1.call-done), kind=kOutput, calls=%fused_computation.8 | convolution fusion | flops 536870912 | bytes 4456448 | tf_op jit(solution)/shard_map/dot_general | solution.py:33
  91.9 0.0 copy-done
  91.9 0.3 copy-done.2
  92.2 0.8 multiply_convert_fusion.2
  93.0 2.7 %fusion.6 = f32[256,4096]{1,0:T(8,128)} fusion(bf16[256,256]{1,0:T(8,128)(2,1)S(1)} %get-tuple-element.9, bf16[1,256,4096]{2,1,0:T(8,128)(2,1)S(1)} %copy-done.1), kind=kOutput, calls=%fused_computation.10 | convolution fusion | flops 536870912 | bytes 6422528 | tf_op jit(solution)/shard_map/dot_general | solution.py:99
  95.7 0.0 reduce-scatter.3.cloned.1.call-update
  95.7 0.0 reduce-scatter.5.cloned.1.call-start
  95.7 2.3 %fusion.11 = f32[256,4096]{1,0:T(8,128)S(1)} fusion(bf16[256,256]{1,0:T(8,128)(2,1)S(1)} %get-tuple-element.10, bf16[1,4096,256]{2,1,0:T(8,128)(2,1)} %param.11), kind=kOutput, calls=%fused_computation.15 | convolution fusion | flops 536870912 | bytes 6422528 | tf_op jit(solution)/shard_map/dot_general | solution.py:33
  98.1 2.1 fusion
  100.2 0.0 copy-start.4
  100.2 0.0 reduce-scatter.5.cloned.1.call-update
  100.2 0.1 reduce_sum.48
  100.3 0.1 copy.28
  100.4 0.5 copy-done.4
  100.8 0.1 copy.29
  100.9 0.2 convert_reduce_fusion.2
  101.1 3.7 %fusion.1 = bf16[1,4096,256]{2,1,0:T(8,128)(2,1)} fusion(bf16[256,256]{1,0:T(8,128)(2,1)S(1)} %get-tuple-element.10, bf16[512,4096]{1,0:T(8,128)(2,1)} %all-gather.2.cloned.1.call-done), kind=kOutput, calls=%fused_computation.5 | convolution fusion | flops 537919488 | bytes 4325376 | tf_op jit(solution)/shard_map/dot_general | solution.py:27
  104.8 45.1 %reduce-scatter.3.cloned.1.call-done = f32[256,512]{1,0:T(8,128)} async-done(((f32[256,4096]{1,0:T(8,128)}), f32[256,512]{1,0:T(8,128)}) %reduce-scatter.3.cloned.1.call-update) | async-done | bytes 524304 | tf_op jit(solution)/shard_map/reduce_scatter | solution.py:100
  149.9 1.1 convert_bitcast_fusion
  150.9 39.3 %reduce-scatter.5.cloned.1.call-done = bf16[256,512]{1,0:T(8,128)(2,1)} async-done(((bf16[256,4096]{1,0:T(8,128)(2,1)}), bf16[256,512]{1,0:T(8,128)(2,1)}) %reduce-scatter.5.cloned.1.call-update) | async-done | bytes 262160 | tf_op jit(solution)/shard_map/reduce_scatter | solution.py:109
  190.2 1.8 pad_maximum_fusion.2
  192.0 11.6 %all-to-all-start.1 = ((bf16[32,16,512]{2,1,0:T(8,128)(2,1)}), bf16[32,16,512]{2,1,0:T(8,128)(2,1)S(1)}, u32[]{:S(2)}, u32[]{:S(2)}) async-start(bf16[32,16,512]{2,1,0:T(8,128)(2,1)} %pad_maximum_fusion.2), calls=%async_computation.3 | async-start | bytes 1048576 | tf_op jit(solution)/shard_map/all_to_all | solution.py:13
  203.6 0.0 copy-start.3
  203.6 3.8 %fusion.3 = bf16[1,256,4096]{2,1,0:T(8,128)(2,1)} fusion(bf16[256,256]{1,0:T(8,128)(2,1)S(1)} %get-tuple-element.9, bf16[512,4096]{1,0:T(8,128)(2,1)} %all-gather.2.cloned.1.call-done), kind=kOutput, calls=%fused_computation.7 | convolution fusion | flops 537919488 | bytes 4325376 | tf_op jit(solution)/shard_map/dot_general | solution.py:27
  207.4 0.0 copy-done.3
  207.4 2.1 fusion.2
  209.5 5.7 %all-to-all-done.1 = bf16[32,16,512]{2,1,0:T(8,128)(2,1)S(1)} async-done(((bf16[32,16,512]{2,1,0:T(8,128)(2,1)}), bf16[32,16,512]{2,1,0:T(8,128)(2,1)S(1)}, u32[]{:S(2)}, u32[]{:S(2)}) %all-to-all-start.1) | async-done | bytes 524320 | tf_op jit(solution)/shard_map/all_to_all | solution.py:13
  215.2 0.1 convert_reduce_fusion
  215.3 0.7 convolution_convert_fusion.6
  216.0 0.7 convolution_convert_fusion.5
  (6 shorter events, 0.1 us)
Async XLA Ops:
  7.2 84.7 %copy-start = (bf16[1,4096,256]{2,1,0:T(8,128)(2,1)S(1)}, bf16[1,4096,256]{2,1,0:T(8,128)(2,1)}, u32[]{:S(2)}) copy-start(bf16[1,4096,256]{2,1,0:T(8,128)(2,1)} %param.12) | copy-start | bytes 6291460
  7.2 79.1 %all-gather.2.cloned.1.call-start = ((), (), s32[]{:S(2)}) async-start(), calls=%async_computation.4 | async-start | bytes 4718592 | tf_op jit(solution)/shard_map/all_gather | solution.py:19
  32.7 117.2 %reduce-scatter.3.cloned.1.call-start = ((), (), s32[]{:S(2)}) async-start(), calls=%async_computation.5 | async-start | bytes 4718592 | tf_op jit(solution)/shard_map/reduce_scatter | solution.py:100
  86.3 3.1 %copy-start.1 = (bf16[1,256,4096]{2,1,0:T(8,128)(2,1)S(1)}, bf16[1,256,4096]{2,1,0:T(8,128)(2,1)}, u32[]{:S(2)}) copy-start(bf16[1,256,4096]{2,1,0:T(8,128)(2,1)} %param.13) | copy-start | bytes 6291460
  89.4 2.8 %copy-start.2 = (bf16[512,4096]{1,0:T(8,128)(2,1)S(1)}, bf16[512,4096]{1,0:T(8,128)(2,1)}, u32[]{:S(2)}) copy-start(bf16[512,4096]{1,0:T(8,128)(2,1)} %all-gather.2.cloned.1.call-done) | copy-start | bytes 12582916
  95.7 94.5 %reduce-scatter.5.cloned.1.call-start = ((), (), s32[]{:S(2)}) async-start(), calls=%async_computation.6 | async-start | bytes 2359296 | tf_op jit(solution)/shard_map/reduce_scatter | solution.py:109
  100.2 0.7 copy-start.4
  192.0 23.2 %all-to-all-start.1 = ((bf16[32,16,512]{2,1,0:T(8,128)(2,1)}), bf16[32,16,512]{2,1,0:T(8,128)(2,1)S(1)}, u32[]{:S(2)}, u32[]{:S(2)}) async-start(bf16[32,16,512]{2,1,0:T(8,128)(2,1)} %pad_maximum_fusion.2), calls=%async_computation.3 | async-start | bytes 1048576 | tf_op jit(solution)/shard_map/all_to_all | solution.py:13
  203.6 3.8 %copy-start.3 = (bf16[512,4096]{1,0:T(8,128)(2,1)S(1)}, bf16[512,4096]{1,0:T(8,128)(2,1)}, u32[]{:S(2)}) copy-start(bf16[512,4096]{1,0:T(8,128)(2,1)} %all-gather.2.cloned.1.call-done) | copy-start | bytes 12582916
Sparse Core Ops, SparseCore 0:
  32.8 53.4 all-gather.1
  95.8 54.0 reduce-scatter.2
  153.0 37.1 reduce-scatter.4
where the time goes:
time: 224 us; the launch traced here: 223 us
  waiting for transfers between devices  144 us (64%)
  matrix products  25 us (11%)
  blocking collectives  20 us (9%)
  between operations  13.9 us (6%)
  starting transfers between devices  11.7 us (5%)
  local copies, waits for them, and re-layouts  4.73 us (2%)
  other arithmetic  4.36 us (2%)
    all_gather x1, waiting for transfers between devices, in_one_piece(): result, at, done = (lax.all_gather(both, axis, axis=dim, tiled=True), 0, [])  53.5 us
    reduce_scatter x1, waiting for transfers between devices, per_device(): lax.psum_scatter(out_term, 'tp', scatter_dimension=1, tiled=True)  45.1 us
    reduce_scatter x1, waiting for transfers between devices, per_device(): lax.psum_scatter(back_term.astype(jnp.bfloat16), 'tp', scatter_dimension=...  39.3 us
    all_to_all x1, blocking collectives, side_by_side(): lax.all_to_all(both, axis, split_axis=split_dim, concat_axis=concat_dim,...  20 us
    all_to_all x1, starting transfers between devices, side_by_side(): lax.all_to_all(both, axis, split_axis=split_dim, concat_axis=concat_dim,...  11.6 us
    dot_general x5, matrix products, contract_rows(): lax.dot_general(left, right, (((0,), (0,)), ((), ())), preferred_element_...  10.1 us
    dot_general x3, matrix products, contract_cols(): lax.dot_general(left, right, (((1,), (1,)), ((), ())), preferred_element_...  6.89 us
    all_to_all x1, waiting for transfers between devices, side_by_side(): lax.all_to_all(both, axis, split_axis=split_dim, concat_axis=concat_dim,...  5.7 us
  transfers between devices with their start and end apart: 4, of which 4 were waited for; matrix products, arithmetic and copies ran while one was open for 7% of the time, Pallas kernels for 0%

commit v1 on v0

v1 whole, which is shorter than its diff:
```python
import functools
import math

import jax
import jax.numpy as jnp
from jax import lax
from jax.experimental import pallas as pl
from jax.experimental.pallas import tpu as pltpu
from jax.sharding import Mesh, PartitionSpec as P


EXPERTS = 8
CAP = 8

EXP_AXES = ("x", "yh", "yl", "c")
TP_AXES = ("za", "zb")
PEERS = ("zb", "x", "yh", "yl")
F32, BF16 = jnp.float32, jnp.bfloat16


def mm(a, b):
    return jnp.dot(a, b, preferred_element_type=F32)


def mm_nt(a, b):
    return lax.dot_general(a, b, (((1,), (1,)), ((), ())), preferred_element_type=F32)


def mm_tn(a, b):
    return lax.dot_general(a, b, (((0,), (0,)), ((), ())), preferred_element_type=F32)


def slot_hits(exp_ref, gate_ref, rows, group):
    n_tok = exp_ref.shape[1]
    r = lax.broadcasted_iota(jnp.int32, (rows, n_tok), 0)
    k, s = r // group, r % CAP
    first, second = exp_ref[0:1, :] == k, exp_ref[1:2, :] == k
    named = (first | second).astype(F32)
    before_of = lax.broadcasted_iota(jnp.int32, (n_tok, n_tok), 0) < lax.broadcasted_iota(
        jnp.int32, (n_tok, n_tok), 1
    )
    before = mm(named.astype(BF16), before_of.astype(F32).astype(BF16))
    hit = jnp.where(before == s.astype(F32), named, 0.0)
    gate = jnp.where(first, gate_ref[0:1, :], 0.0) + jnp.where(second, gate_ref[1:2, :], 0.0)
    return hit, hit * gate


def lane_shift(n_tok, by):
    row = lax.broadcasted_iota(jnp.int32, (n_tok, 2 * n_tok), 0)
    lane = lax.broadcasted_iota(jnp.int32, (n_tok, 2 * n_tok), 1)
    return (lane == row + by).astype(F32).astype(BF16)


def route_kernel(exp_ref, gate_ref, x_ref, g_ref, scale_ref, high_ref, low_ref, hit_ref, *, group):
    n_tok = exp_ref.shape[1]
    left, right = lane_shift(n_tok, 0), lane_shift(n_tok, n_tok)
    hit, weighted = slot_hits(exp_ref, gate_ref, EXPERTS * CAP, CAP)
    x_ref[...] = mm(hit.astype(BF16), left).astype(BF16)
    g_ref[...] = mm(hit.astype(BF16), right).astype(BF16)
    scale_ref[...] = jnp.broadcast_to(jnp.sum(weighted, axis=1, keepdims=True), scale_ref.shape)

    rows = EXPERTS * group
    hit, weighted = slot_hits(exp_ref, gate_ref, rows, group)
    high = weighted.astype(BF16)
    low = (weighted - high.astype(F32)).astype(BF16)
    same = (
        lax.broadcasted_iota(jnp.int32, (rows, rows), 0)
        == lax.broadcasted_iota(jnp.int32, (rows, rows), 1)
    )
    same = same.astype(F32).astype(BF16)
    for ref, table, side in ((high_ref, high, left), (low_ref, low, left), (hit_ref, hit, right)):
        ref[...] = mm_tn(mm(table.astype(BF16), side).astype(BF16), same).astype(BF16)


def dispatch_kernel(x_ref, g_ref, scale_ref, in_ref, out_ref):
    zb, _, yl, _, _ = out_ref.shape
    blocks, _, fblk = in_ref.shape
    for b in range(blocks):
        x = mm(x_ref[...], in_ref[b])
        g = mm(g_ref[...], in_ref[b]) * scale_ref[:, :1]
        for part, value in enumerate((x, g)):
            value = value.reshape(EXPERTS, CAP, fblk).astype(BF16)
            at = (part * blocks + b) * fblk
            for i in range(zb):
                for j in range(yl):
                    out_ref[i, :, j, :, at : at + fblk] = value


def hidden(got_ref, w1_ref, w3_ref, w2_ref, act_ref, d1_ref, d3_ref, fblk):
    pairs, _, wide = got_ref.shape
    half = wide // 2
    first = second = third = 0.0
    for p in range(pairs):
        for b in range(half // fblk):
            x = got_ref[p, :, b * fblk : (b + 1) * fblk]
            g = got_ref[p, :, half + b * fblk : half + (b + 1) * fblk]
            at = (b * pairs + p) * fblk
            first = first + mm(x, w1_ref[at : at + fblk, :])
            second = second + mm(x, w3_ref[at : at + fblk, :])
            third = third + mm_nt(g, w2_ref[:, at : at + fblk])
    sig = jax.nn.sigmoid(first)
    act_ref[...] = (first * sig * second).astype(BF16)
    d1_ref[...] = (third * second * sig * (1.0 + first * (1.0 - sig))).astype(BF16)
    d3_ref[...] = (third * first * sig).astype(BF16)


def back_x(d1_ref, d3_ref, w1_ref, w3_ref, out_ref, fblk):
    pairs, _, wide = out_ref.shape
    for p in range(pairs):
        for b in range(wide // fblk):
            at = (b * pairs + p) * fblk
            value = mm_nt(d1_ref[...], w1_ref[at : at + fblk, :])
            value = value + mm_nt(d3_ref[...], w3_ref[at : at + fblk, :])
            out_ref[p, :, b * fblk : (b + 1) * fblk] = value.astype(BF16)


def back_y(act_ref, w2_ref, out_ref, fblk):
    pairs, _, wide = out_ref.shape
    for p in range(pairs):
        for b in range(wide // fblk):
            at = (b * pairs + p) * fblk
            value = mm(act_ref[...], w2_ref[:, at : at + fblk])
            out_ref[p, :, b * fblk : (b + 1) * fblk] = value.astype(BF16)


def own_kernel(got, w1, w3, w2, act, d1, d3, y, dx, *, fblk):
    hidden(got, w1, w3, w2, act, d1, d3, fblk)
    back_y(act, w2, y, fblk)
    back_x(d1, d3, w1, w3, dx, fblk)


def other_y_kernel(got, w1, w3, w2, _, act, d1, d3, y, *, fblk):
    hidden(got, w1, w3, w2, act, d1, d3, fblk)
    back_y(act, w2, y, fblk)


def other_x_kernel(d1, d3, w1, w3, dx, *, fblk):
    back_x(d1, d3, w1, w3, dx, fblk)


def add_kernel(y0, y1, dx0, dx1, out_ref, total, sems):
    pairs, _, wide = y0.shape
    copies = []
    for part, (mine, theirs) in enumerate(((y0, y1), (dx0, dx1))):
        for p in range(pairs):
            lanes = slice(part * wide, (part + 1) * wide)
            total[p, :, lanes] = (mine[p].astype(F32) + theirs[p].astype(F32)).astype(BF16)
            copies.append(
                pltpu.make_async_copy(
                    total.at[p, :, lanes], out_ref.at[p, :, lanes], sems.at[part * pairs + p]
                )
            )
            copies[-1].start()
    for copy in copies:
        copy.wait()


def weight_grad_kernel(got0, got1, a0, a1, b0, b1, c0, c1, gg_ref, gu_ref, gd_ref, done_ref):
    t = pl.program_id(0)
    pairs, _, wide = got0.shape
    fblk = gg_ref.shape[0]
    p, b = lax.rem(t, pairs), lax.div(t, pairs)
    x_at = pl.ds(pl.multiple_of(b * fblk, fblk), fblk)
    g_at = pl.ds(pl.multiple_of(wide // 2 + b * fblk, fblk), fblk)
    both = lambda u, v: jnp.concatenate([u, v], axis=0)
    x = both(got0[p, :, x_at], got1[p, :, x_at])
    g = both(got0[p, :, g_at], got1[p, :, g_at])
    gg_ref[...] = mm_tn(x, both(b0[...], b1[...])).astype(BF16)
    gu_ref[...] = mm_tn(x, both(c0[...], c1[...])).astype(BF16)
    gd_ref[...] = mm_tn(both(a0[...], a1[...]), g).astype(BF16)
    done_ref[...] = jnp.zeros_like(done_ref)


def combine_kernel(high_ref, low_ref, hit_ref, home_ref, _, out_ref):
    pairs, _, wide = home_ref.shape
    blocks, _, fblk = out_ref.shape
    for b in range(blocks):
        out = 0.0
        for p in range(pairs):
            y = home_ref[p, :, b * fblk : (b + 1) * fblk]
            dx = home_ref[p, :, wide // 2 + b * fblk : wide // 2 + (b + 1) * fblk]
            out = out + mm(high_ref[...], y) + mm(low_ref[...], y) + mm(hit_ref[...], dx)
        out_ref[b] = out.astype(BF16)


VMEM = pl.BlockSpec(memory_space=pltpu.VMEM)
HBM = pl.BlockSpec(memory_space=pltpu.HBM)


def call(kernel, ins, outs, grid=(), out_specs=None, scratch=(), flops=0, nbytes=0):
    return pl.pallas_call(
        kernel,
        grid=grid,
        in_specs=[VMEM] * ins if isinstance(ins, int) else ins,
        out_specs=out_specs or [VMEM] * len(outs),
        out_shape=[jax.ShapeDtypeStruct(shape, dtype) for shape, dtype in outs],
        scratch_shapes=list(scratch),
        compiler_params=pltpu.CompilerParams(vmem_limit_bytes=24 * 1024 * 1024),
        cost_estimate=pl.CostEstimate(flops=flops, bytes_accessed=nbytes, transcendentals=0),
    )


def per_device(tokens, cotangent, experts, gates, w_gate, w_up, w_down):
    za, zb, yl = (lax.axis_size(a) for a in ("za", "zb", "yl"))
    peers = math.prod(lax.axis_size(a) for a in PEERS)
    n_tok, fblk = tokens.shape
    w1, w3, w2 = w_gate[0], w_up[0], w_down[0]
    width, hid = w1.shape
    wide = za * fblk
    rows = peers // zb * CAP
    swap = [(0, 1), (1, 0)]
    fb = dict(fblk=fblk)

    both = jnp.concatenate([tokens, cotangent], axis=0)
    spread = jnp.broadcast_to(both[None], (za,) + both.shape)
    mine = lax.all_to_all(spread, "za", 0, 0, tiled=True)
    table = ((2 * n_tok, EXPERTS * yl * CAP), BF16)
    pick = ((EXPERTS * CAP, 2 * n_tok), BF16)
    pick_x, pick_g, scale, high, low, hit = call(
        functools.partial(route_kernel, group=yl * CAP),
        2,
        [pick, pick, ((EXPERTS * CAP, 128), F32)] + [table] * 3,
    )(experts.T, gates.T)

    (send,) = call(dispatch_kernel, 4, [((zb, EXPERTS, yl, CAP, 2 * wide), BF16)])(
        pick_x, pick_g, scale, mine
    )
    send = send.reshape(peers, CAP, 2 * wide)
    got0 = lax.all_to_all(send, PEERS, 0, 0, tiled=True).reshape(zb, rows, 2 * wide)

    got1 = lax.ppermute(got0, "c", swap)
    product = 2 * rows * width * hid
    square = [((rows, hid), BF16)] * 3
    piece = ((zb, rows, wide), BF16)
    a0, b0, c0, y0, dx0 = call(
        functools.partial(own_kernel, **fb), 4, square + [piece] * 2, flops=6 * product
    )(got0, w1, w3, w2)
    a1, b1, c1, y1 = call(
        functools.partial(other_y_kernel, **fb), 5, square + [piece], flops=4 * product
    )(got1, w1, w3, w2, a0)
    y1 = lax.ppermute(y1, "c", swap)
    (dx1,) = call(
        functools.partial(other_x_kernel, **fb), 4, [piece], flops=2 * product
    )(b1, c1, w1, w3)
    dx1 = lax.ppermute(dx1, "c", swap)

    full = (zb, rows, 2 * wide)
    (ours,) = call(
        add_kernel,
        4,
        [(full, BF16)],
        out_specs=[HBM],
        scratch=[pltpu.VMEM(full, BF16), pltpu.SemaphoreType.DMA((2 * zb,))],
    )(y0, y1, dx0, dx1)
    home = lax.all_to_all(ours.reshape(peers, CAP, 2 * wide), PEERS, 0, 0, tiled=True)

    tall = pl.BlockSpec((fblk, hid), lambda t: (t, 0))
    flat = pl.BlockSpec((hid, fblk), lambda t: (0, t))
    grad_gate, grad_up, grad_down, done = call(
        weight_grad_kernel,
        8,
        [((width, hid), BF16)] * 2 + [((hid, width), BF16), ((8, 128), F32)],
        grid=(width // fblk,),
        out_specs=[tall, tall, flat, pl.BlockSpec((8, 128), lambda t: (0, 0))],
        flops=6 * product,
        nbytes=6 * width * hid,
    )(got0, got1, a0, a1, b0, b1, c0, c1)

    (mixed,) = call(combine_kernel, 5, [((za, 2 * n_tok, fblk), BF16)])(
        high, low, hit, home.reshape(zb, EXPERTS * yl * CAP, 2 * wide), done
    )
    parts = lax.all_to_all(mixed, "za", 0, 0, tiled=True)
    total = jnp.sum(parts.astype(F32), axis=0)
    output, input_grad = total[:n_tok].astype(BF16), total[n_tok:].astype(BF16)
    return output, input_grad, grad_gate[None], grad_up[None], grad_down[None]


def solution(mesh):
    group = mesh.shape["exp"] // EXPERTS
    shape = (EXPERTS // 2, 2, group // 2, 2, mesh.shape["tp"] // 2, 2)
    fine = Mesh(mesh.devices.reshape(shape), EXP_AXES + TP_AXES)
    spec = (
        P(EXP_AXES, TP_AXES),
        P(EXP_AXES, TP_AXES),
        P(EXP_AXES, None),
        P(EXP_AXES, None),
        P(EXP_AXES, None, TP_AXES),
        P(EXP_AXES, None, TP_AXES),
        P(EXP_AXES, TP_AXES, None),
    )
    out = (spec[0], spec[1], spec[4], spec[5], spec[6])
    return jax.shard_map(per_device, mesh=fine, in_specs=spec, out_specs=out, check_vma=False)
```

time: 224 us -> 117 us (0.52)
  the two profiles are of different devices: /device:TPU:1 before, /device:TPU:34 now
where the time goes in v1:
time: 117 us; the launch traced here: 116 us
  blocking collectives  46.2 us (39%)
  waiting for transfers between devices  32.8 us (28%)
  Pallas kernels  15.6 us (13%)
  starting transfers between devices  14 us (12%)
  local copies, waits for them, and re-layouts  5.89 us (5%)
    all_to_all x1, blocking collectives, per_device(): lax.all_to_all(send, PEERS, 0, 0, tiled=True).reshape(zb, rows, 2 * wide)  33 us
    all_to_all x1, waiting for transfers between devices, per_device(): lax.all_to_all(ours.reshape(peers, CAP, 2 * wide), PEERS, 0, 0, tiled=True)  20.7 us
    all_to_all x1, blocking collectives, per_device(): parts = lax.all_to_all(mixed, 'za', 0, 0, tiled=True)  13.2 us
    all_to_all x1, waiting for transfers between devices, per_device(): mine = lax.all_to_all(spread, 'za', 0, 0, tiled=True)  8.11 us
    all_to_all x1, starting transfers between devices, per_device(): mine = lax.all_to_all(spread, 'za', 0, 0, tiled=True)  7.56 us
    all_to_all x1, starting transfers between devices, per_device(): lax.all_to_all(ours.reshape(peers, CAP, 2 * wide), PEERS, 0, 0, tiled=True)  5.83 us
    pallas_call x1, Pallas kernels, per_device(): call(weight_grad_kernel, 8, [((width, hid), BF16)] * 2 + [((hid, width),...  5.29 us
    unnamed x18, local copies, waits for them, and re-layouts  4.56 us
  transfers between devices with their start and end apart: 5, of which 5 were waited for; matrix products, arithmetic and copies ran while one was open for 0% of the time, Pallas kernels for 8%

profile of v1, /device:TPU:34, one launch (start us, length us, event | category | flops | bytes accessed | tf_op | source)
XLA Modules:
  0.0 116.1 jit_solution(8604912856862496850)
XLA Ops:
  0.6 0.8 pad_maximum_fusion
  1.4 0.7 broadcast_in_dim.15
  2.1 7.6 %all-to-all-start = ((bf16[4,56,512]{2,1,0:T(8,128)(2,1)}), bf16[4,56,512]{2,1,0:T(8,128)(2,1)S(1)}, u32[]{:S(2)}, u32[]{:S(2)}) async-start(bf16[4,56,512]{2,1,0:T(8,128)(2,1)} %broadcast_in_dim.15), calls=%async_computation | async-start | bytes 458752 | tf_op jit(solution)/shard_map/all_to_all | solution.py:216
  9.7 0.0 copy-start.7
  9.7 0.7 copy-done.7
  10.4 0.0 copy-start.8
  10.4 0.7 copy-done.8
  11.0 0.6 shard_map.110
  11.6 8.1 %all-to-all-done.in_ref = bf16[4,56,512]{2,1,0:T(8,128)(2,1)S(1)} async-done(((bf16[4,56,512]{2,1,0:T(8,128)(2,1)}), bf16[4,56,512]{2,1,0:T(8,128)(2,1)S(1)}, u32[]{:S(2)}, u32[]{:S(2)}) %all-to-all-start) | async-done | bytes 229408 | tf_op jit(solution)/shard_map/all_to_all | solution.py:216
  19.7 0.0 copy-start.4
  19.7 0.3 shard_map.111
  20.1 0.0 copy-start
  20.1 0.0 copy-start.1
  20.1 33.0 %all_to_all.20 = bf16[32,8,4096]{2,1,0:T(8,128)(2,1)S(1)} all-to-all(bf16[32,8,4096]{2,1,0:T(8,128)(2,1)S(1)} %bitcast.19), channel_id=1, replica_groups=mesh['x'=4,'yh'=2,'yl'=2,'c'=2,'za'=4,'zb'=2] {'zb','x','yh','yl'}, dimensions={0} | all-to-all | bytes 4194304 | tf_op jit(solution)/shard_map/all_to_all | solution.py:229
  53.1 0.0 copy-start.2
  53.1 0.0 collective-permute-start
  53.1 0.0 copy-done.4
  53.1 0.0 copy-done
  53.1 0.0 copy-done.1
  53.1 3.8 %shard_map.112 = (bf16[128,256]{1,0:T(8,128)(2,1)S(1)}, bf16[128,256]{1,0:T(8,128)(2,1)S(1)}, bf16[128,256]{1,0:T(8,128)(2,1)S(1)}, bf16[2,128,2048]{2,1,0:T(8,128)(2,1)S(1)}, bf16[2,128,2048]{2,1,0:T(8,128)(2,1)S(1)}) custom-call(bf16[2,128,4096]{2,1,0:T(8,128)(2,1)S(1)} %bitcast.21, bf16[4096,256]{1,0:T(8,128)(2,1)S(1)} %bitcast.12, ...), custom_call_target="tpu_custom_call" | custom-call | flops 1610612736 | tf_op jit(solution)/shard_map/pallas_call | solution.py:235
  56.9 0.0 copy-done.2
  56.9 0.3 collective-permute-done.got.got1
  57.2 0.0 copy-start.5
  57.2 2.1 %shard_map.113 = (bf16[128,256]{1,0:T(8,128)(2,1)S(1)}, bf16[128,256]{1,0:T(8,128)(2,1)S(1)}, bf16[128,256]{1,0:T(8,128)(2,1)S(1)}, bf16[2,128,2048]{2,1,0:T(8,128)(2,1)S(1)}) custom-call(bf16[2,128,4096]{2,1,0:T(8,128)(2,1)S(1)} %collective-permute-done.got.got1, bf16[4096,256]{1,0:T(8,128)(2,1)S(1)} %bitcast.13, bf16[4096,256]{1,0:T(8,128)(2,1)S(1)} %bitcast.16, ...), custom_call_target="tpu_custom_call" | custom-call | flops 1073741824 | tf_op jit(solution)/shard_map/pallas_call | solution.py:238
  59.4 0.0 copy-done.5
  59.4 1.5 %shard_map.114 = bf16[2,128,2048]{2,1,0:T(8,128)(2,1)S(1)} custom-call(bf16[128,256]{1,0:T(8,128)(2,1)S(1)} %get-tuple-element.34.d1.b1, bf16[128,256]{1,0:T(8,128)(2,1)S(1)} %get-tuple-element.35.d3.c1, bf16[4096,256]{1,0:T(8,128)(2,1)S(1)} %bitcast.14, bf16[4096,256]{1,0:T(8,128)(2,1)S(1)} %bitcast.17), custom_call_target="tpu_custom_call" | custom-call | flops 536870912 | tf_op jit(solution)/shard_map/pallas_call | solution.py:242
  60.9 0.3 collective-permute-start.2
  61.1 0.3 collective-permute-start.1
  61.5 2.1 %collective-permute-done.2.dx1 = bf16[2,128,2048]{2,1,0:T(8,128)(2,1)S(1)} collective-permute-done((bf16[2,128,2048]{2,1,0:T(8,128)(2,1)S(1)}, bf16[2,128,2048]{2,1,0:T(8,128)(2,1)S(1)}, u32[]{:S(2)}, u32[]{:S(2)}) %collective-permute-start.2) | collective-permute-done | bytes 1048608 | tf_op jit(solution)/shard_map/ppermute | solution.py:245
  63.6 1.5 %collective-permute-done.1.y1 = bf16[2,128,2048]{2,1,0:T(8,128)(2,1)S(1)} collective-permute-done((bf16[2,128,2048]{2,1,0:T(8,128)(2,1)S(1)}, bf16[2,128,2048]{2,1,0:T(8,128)(2,1)S(1)}, u32[]{:S(2)}, u32[]{:S(2)}) %collective-permute-start.1) | collective-permute-done | bytes 1048608 | tf_op jit(solution)/shard_map/ppermute | solution.py:241
  65.1 1.5 %shard_map.115 = bf16[2,128,4096]{2,1,0:T(8,128)(2,1)} custom-call(bf16[2,128,2048]{2,1,0:T(8,128)(2,1)S(1)} %get-tuple-element.30.y0, bf16[2,128,2048]{2,1,0:T(8,128)(2,1)S(1)} %collective-permute-done.1.y1, bf16[2,128,2048]{2,1,0:T(8,128)(2,1)S(1)} %get-tuple-element.33.dx0, bf16[2,128,2048]{2,1,0:T(8,128)(2,1)S(1)} %collective-permute-done.2.dx1), custom_call_target="tpu_custom_call" | custom-call | tf_op jit(solution)/shard_map/pallas_call | solution.py:248
  66.6 5.8 %all-to-all-start.2 = ((bf16[32,8,4096]{2,1,0:T(8,128)(2,1)}), bf16[32,8,4096]{2,1,0:T(8,128)(2,1)S(1)}, u32[]{:S(2)}, u32[]{:S(2)}) async-start(bf16[32,8,4096]{2,1,0:T(8,128)(2,1)} %bitcast.7), calls=%async_computation.2 | async-start | bytes 4194304 | tf_op jit(solution)/shard_map/all_to_all | solution.py:255
  72.5 0.0 copy-start.3
  72.5 1.6 %copy-done.3 = bf16[32,8,4096]{2,1,0:T(8,128)(2,1)S(1)} copy-done((bf16[32,8,4096]{2,1,0:T(8,128)(2,1)S(1)}, bf16[32,8,4096]{2,1,0:T(8,128)(2,1)}, u32[]{:S(2)}) %copy-start.3) | copy-done | bytes 2097176
  74.1 0.0 copy-start.6
  74.1 1.6 %copy-done.6 = bf16[2,128,4096]{2,1,0:T(8,128)(2,1)S(1)} copy-done((bf16[2,128,4096]{2,1,0:T(8,128)(2,1)S(1)}, bf16[2,128,4096]{2,1,0:T(8,128)(2,1)}, u32[]{:S(2)}) %copy-start.6) | copy-done | bytes 2097176
  75.7 5.3 %shard_map.116 = (bf16[4096,256]{1,0:T(8,128)(2,1)}, bf16[4096,256]{1,0:T(8,128)(2,1)}, bf16[256,4096]{1,0:T(8,128)(2,1)}, f32[8,128]{1,0:T(8,128)S(1)}) custom-call(bf16[2,128,4096]{2,1,0:T(8,128)(2,1)S(1)} %bitcast.22, bf16[2,128,4096]{2,1,0:T(8,128)(2,1)S(1)} %copy-done.6, bf16[128,256]{1,0:T(8,128)(2,1)S(1)} %get-tuple-element.31._.a0, ...), custom_call_target="tpu_custom_call" | custom-call | flops 1610612736 | bytes 6291456 | tf_op jit(solution)/shard_map/pallas_call | solution.py:259
  80.9 20.7 %all-to-all-done.2 = bf16[32,8,4096]{2,1,0:T(8,128)(2,1)S(1)} async-done(((bf16[32,8,4096]{2,1,0:T(8,128)(2,1)}), bf16[32,8,4096]{2,1,0:T(8,128)(2,1)S(1)}, u32[]{:S(2)}, u32[]{:S(2)}) %all-to-all-start.2) | async-done | bytes 2097184 | tf_op jit(solution)/shard_map/all_to_all | solution.py:255
  101.6 0.6 shard_map.117
  102.2 13.2 %all_to_all.21 = bf16[4,56,512]{2,1,0:T(8,128)(2,1)S(1)} all-to-all(bf16[4,56,512]{2,1,0:T(8,128)(2,1)S(1)} %shard_map.117), channel_id=1, replica_groups=mesh['x'=4,'yh'=2,'yl'=2,'c'=2,'za'=4,'zb'=2] {'za'}, dimensions={0} | all-to-all | bytes 458752 | tf_op jit(solution)/shard_map/all_to_all | solution.py:272
  115.5 0.6 fusion
  (1 shorter events, 0.0 us)
Async XLA Ops:
  2.1 17.6 %all-to-all-start = ((bf16[4,56,512]{2,1,0:T(8,128)(2,1)}), bf16[4,56,512]{2,1,0:T(8,128)(2,1)S(1)}, u32[]{:S(2)}, u32[]{:S(2)}) async-start(bf16[4,56,512]{2,1,0:T(8,128)(2,1)} %broadcast_in_dim.15), calls=%async_computation | async-start | bytes 458752 | tf_op jit(solution)/shard_map/all_to_all | solution.py:216
  9.7 0.7 copy-start.7
  10.4 0.7 copy-start.8
  19.7 33.3 %copy-start.4 = (bf16[1,256,4096]{2,1,0:T(8,128)(2,1)S(1)}, bf16[1,256,4096]{2,1,0:T(8,128)(2,1)}, u32[]{:S(2)}) copy-start(bf16[1,256,4096]{2,1,0:T(8,128)(2,1)} %param.13) | copy-start | bytes 6291460
  20.1 33.0 %copy-start = (bf16[1,4096,256]{2,1,0:T(8,128)(2,1)S(1)}, bf16[1,4096,256]{2,1,0:T(8,128)(2,1)}, u32[]{:S(2)}) copy-start(bf16[1,4096,256]{2,1,0:T(8,128)(2,1)} %param.11) | copy-start | bytes 6291460
  20.1 33.0 %copy-start.1 = (bf16[1,4096,256]{2,1,0:T(8,128)(2,1)S(1)}, bf16[1,4096,256]{2,1,0:T(8,128)(2,1)}, u32[]{:S(2)}) copy-start(bf16[1,4096,256]{2,1,0:T(8,128)(2,1)} %param.12) | copy-start | bytes 6291460
  53.1 3.8 %copy-start.2 = (bf16[32,8,4096]{2,1,0:T(8,128)(2,1)}, bf16[32,8,4096]{2,1,0:T(8,128)(2,1)S(1)}, u32[]{:S(2)}) copy-start(bf16[32,8,4096]{2,1,0:T(8,128)(2,1)S(1)} %all_to_all.20) | copy-start | bytes 6291460
  53.1 4.2 %collective-permute-start = (bf16[2,128,4096]{2,1,0:T(8,128)(2,1)S(1)}, bf16[2,128,4096]{2,1,0:T(8,128)(2,1)S(1)}, u32[]{:S(2)}, u32[]{:S(2)}) collective-permute-start(bf16[2,128,4096]{2,1,0:T(8,128)(2,1)S(1)} %bitcast.20), channel_id=1, source_target_pairs={{0,8},{8,0},{1,9},{9,1},{2,10},{10,2},{3,11},{11,3},{4,12},{12,4},... | collective-permute-start | bytes 6291464 | tf_op jit(solution)/shard_map/ppermute | solution.py:231
  57.2 2.1 %copy-start.5 = (bf16[2,128,4096]{2,1,0:T(8,128)(2,1)}, bf16[2,128,4096]{2,1,0:T(8,128)(2,1)S(1)}, u32[]{:S(2)}) copy-start(bf16[2,128,4096]{2,1,0:T(8,128)(2,1)S(1)} %collective-permute-done.got.got1) | copy-start | bytes 6291460
  60.9 2.7 %collective-permute-start.2 = (bf16[2,128,2048]{2,1,0:T(8,128)(2,1)S(1)}, bf16[2,128,2048]{2,1,0:T(8,128)(2,1)S(1)}, u32[]{:S(2)}, u32[]{:S(2)}) collective-permute-start(bf16[2,128,2048]{2,1,0:T(8,128)(2,1)S(1)} %shard_map.114), channel_id=1, source_target_pairs={{0,8},{8,0},{1,9},{9,1},{2,10},{10,2},{3,11},{11,3},{4,12},{12,4},... | collective-permute-start | bytes 3145736 | tf_op jit(solution)/shard_map/ppermute | solution.py:245
  61.1 4.0 %collective-permute-start.1 = (bf16[2,128,2048]{2,1,0:T(8,128)(2,1)S(1)}, bf16[2,128,2048]{2,1,0:T(8,128)(2,1)S(1)}, u32[]{:S(2)}, u32[]{:S(2)}) collective-permute-start(bf16[2,128,2048]{2,1,0:T(8,128)(2,1)S(1)} %get-tuple-element.32), channel_id=1, source_target_pairs={{0,8},{8,0},{1,9},{9,1},{2,10},{10,2},{3,11},{11,3},{4,12},{12,4},... | collective-permute-start | bytes 3145736 | tf_op jit(solution)/shard_map/ppermute | solution.py:241
  66.6 35.0 %all-to-all-start.2 = ((bf16[32,8,4096]{2,1,0:T(8,128)(2,1)}), bf16[32,8,4096]{2,1,0:T(8,128)(2,1)S(1)}, u32[]{:S(2)}, u32[]{:S(2)}) async-start(bf16[32,8,4096]{2,1,0:T(8,128)(2,1)} %bitcast.7), calls=%async_computation.2 | async-start | bytes 4194304 | tf_op jit(solution)/shard_map/all_to_all | solution.py:255
  72.5 1.6 %copy-start.3 = (bf16[32,8,4096]{2,1,0:T(8,128)(2,1)S(1)}, bf16[32,8,4096]{2,1,0:T(8,128)(2,1)}, u32[]{:S(2)}) copy-start(bf16[32,8,4096]{2,1,0:T(8,128)(2,1)} %copy-done.2) | copy-start | bytes 6291460
  74.1 1.6 %copy-start.6 = (bf16[2,128,4096]{2,1,0:T(8,128)(2,1)S(1)}, bf16[2,128,4096]{2,1,0:T(8,128)(2,1)}, u32[]{:S(2)}) copy-start(bf16[2,128,4096]{2,1,0:T(8,128)(2,1)} %copy-done.5) | copy-start | bytes 6291460
